TPU v7x, 256 devices: a whole 4x4x8 slice. The times are simulated.
256 devices in a mesh: gx: 4 (over x_hi, core), gy: 8 (over y, x_lo), gz: 8 (over z).
Axes of the slice: x: 4 (x_hi: 2, x_lo: 2; x = x_hi * 2 + x_lo), y: 4, z: 8, core: 2. Of those that a mesh axis runs over, the one named last changes fastest.
Arguments:
- node_feats: bfloat16 [64, 128, 256, 128], P('gx', 'gy', 'gz'), may hold values from -6 to 6
- node_type: int32 [64, 128, 256], P('gx', 'gy', 'gz'), may hold values from 0 to 3
- boundary_code: int32 [64, 128, 256], P('gx', 'gy', 'gz'), may hold values from 0 to 2
- wall_flag: int32 [64, 128, 256], P('gx', 'gy', 'gz'), may hold values from 0 to 1, as said below
- type_table: float32 [4, 128], replicated, may hold values from -3 to 3
- boundary_table: float32 [3, 128], replicated, may hold values from -3 to 3
- edge_self: bfloat16 [2, 128, 128], replicated, may hold values from -0.5 to 0.5
- edge_neighbour: bfloat16 [2, 128, 128], replicated, may hold values from -0.5 to 0.5
- edge_bias: float32 [2, 6, 128], replicated, may hold values from -3 to 3
- edge_out: bfloat16 [2, 128, 128], replicated, may hold values from -0.5 to 0.5
- node_self: bfloat16 [2, 128, 128], replicated, may hold values from -0.5 to 0.5
- node_aggregate: bfloat16 [2, 128, 128], replicated, may hold values from -0.5 to 0.5
- node_out: bfloat16 [2, 128, 128], replicated, may hold values from -0.5 to 0.5
- node_gain: float32 [2, 128], replicated, may hold values from 0.25 to 1.75
Outputs:
- latent: bfloat16 [64, 128, 256, 128], P('gx', 'gy', 'gz')
- wall_mean: float32 [128], replicated
Inputs may be any that keep to these rules, and one draw needn't show every extreme that they name: Every node whose wall-normal index is 0 or 127 has wall_flag 1.
All inputs are finite; a program needn't handle non-finite values.
Results may differ from a plain program's by a relative error of at most 0.012.
Values may be sent and summed in bfloat16 or wider, within the bound.
A program may use at most 128 MiB of HBM per device.

v0:
```python
import functools

import jax
import jax.numpy as jnp
from jax import lax
from jax.experimental import pallas as pl
from jax.experimental.pallas import tpu as pltpu
from jax.sharding import PartitionSpec as P

MESH = pl.DeviceIdType.MESH
AXES = ("gx", "gy", "gz")
EPSILON = 1e-05
BF = jnp.bfloat16
F32 = jnp.float32
PITCH = 48
FIRST = 8


def kernel(
    sizes,
    dims,
    feats,
    ntype,
    bcode,
    wflag,
    ttab,
    btab,
    eself,
    enbr,
    ebias,
    eout,
    nself,
    nagg,
    nout,
    ngain,
    out_lat,
    out_wall,
    lat,
    selfp,
    sb,
    sz,
    hs,
    flag_t,
    zsend,
    zrecv,
    w_sn,
    w_pre,
    w_out,
    bias,
    wall,
    red,
    in_sem,
    out_sem,
    send_sem,
    recv_sem,
    rsend_sem,
    rrecv_sem,
):
    nx, ny, nz, h = dims
    gx, gy, gz = (lax.axis_index(a) for a in AXES)
    here = {"gx": gx, "gy": gy, "gz": gz}

    load = pltpu.make_async_copy(feats, lat, in_sem)
    load.start()
    barrier = pltpu.get_barrier_semaphore()
    peers = 0
    for a in AXES:
        for k in range(1, sizes[a]):
            pl.semaphore_signal(
                barrier,
                inc=1,
                device_id={a: lax.rem(here[a] + k, sizes[a])},
                device_id_type=MESH,
            )
            peers += 1

    for l in range(2):
        w_sn[l, :, :h] = (eself[l].astype(F32) * 0.5).astype(BF)
        w_sn[l, :, h:] = (enbr[l].astype(F32) * 0.5).astype(BF)
        w_pre[l, :h, :] = (nself[l].astype(F32) * 0.5).astype(BF)
        folded = jnp.dot(eout[l], nagg[l], preferred_element_type=F32)
        w_pre[l, h:, :] = (folded * 0.5).astype(BF)
        w = nout[l].astype(F32)
        w_out[l] = (w - jnp.mean(w, axis=1, keepdims=True)).astype(BF)
        for d in range(6):
            row = ebias[l, d : d + 1, :] * 0.5
            bias[l, d] = jnp.broadcast_to(row, (nz, h)).astype(BF)
    wall[...] = jnp.zeros_like(wall)
    zero = jnp.zeros((nx, 1, nz, h), BF)

    @pl.when(gy == 0)
    def _():
        sb[0, 1 : nx + 1, 0:1] = zero
        sb[1, 1 : nx + 1, 0:1] = zero

    @pl.when(gy == sizes["gy"] - 1)
    def _():
        sb[0, 1 : nx + 1, ny + 1 : ny + 2] = zero
        sb[1, 1 : nx + 1, ny + 1 : ny + 2] = zero

    def store_parts(r, x0, cx, y0, cy, both):
        s = both[:, h:].reshape(cx, cy, nz, h)
        selfp[pl.ds(x0, cx), pl.ds(y0, cy)] = both[:, :h].astype(BF).reshape(cx, cy, nz, h)
        sb[r, pl.ds(x0 + 1, cx), pl.ds(y0 + 1, cy)] = s.astype(BF)
        sz[r, pl.ds(x0, cx), pl.ds(y0, cy), FIRST : FIRST + nz, :] = s

    load.wait()

    @pl.loop(0, nx)
    def _(x):
        code = (ntype[x] + 4 * bcode[x]).astype(F32).T
        flag_t[x] = wflag[x].astype(F32).T
        for y in range(ny):
            c = jnp.broadcast_to(code[:, y : y + 1], (nz, h))
            which = c
            extra = jnp.broadcast_to(btab[0:1, :], (nz, h))
            for b in range(1, 3):
                hit = c >= 4.0 * b
                extra = jnp.where(hit, btab[b : b + 1, :], extra)
                which = jnp.where(hit, c - 4.0 * b, which)
            kind = jnp.broadcast_to(ttab[0:1, :], (nz, h))
            for t in range(1, 4):
                kind = jnp.where(which >= 1.0 * t, ttab[t : t + 1, :], kind)
            lat[x, y] = (lat[x, y].astype(F32) + kind + extra).astype(BF)
        both = jnp.dot(
            lat[x].reshape(ny * nz, h), w_sn[0], preferred_element_type=F32
        )
        store_parts(0, x, 1, 0, ny, both)

    def copies(r):
        up = {a: lax.rem(here[a] + 1, sizes[a]) for a in AXES}
        down = {a: lax.rem(here[a] + sizes[a] - 1, sizes[a]) for a in AXES}
        own = lambda f, *at: f.at[(r,) + at]
        rows_x, rows_y = pl.ds(1, nx), pl.ds(1, ny)
        plans = (
            ("gx", up, own(sb, nx, rows_y), own(sb, 0, rows_y)),
            ("gx", down, own(sb, 1, rows_y), own(sb, nx + 1, rows_y)),
            ("gy", up, own(sb, rows_x, ny), own(sb, rows_x, 0)),
            ("gy", down, own(sb, rows_x, 1), own(sb, rows_x, ny + 1)),
            ("gz", up, own(zsend, 1), own(zrecv, 0)),
            ("gz", down, own(zsend, 0), own(zrecv, 1)),
        )
        return [
            pltpu.make_async_remote_copy(
                src_ref=src,
                dst_ref=dst,
                send_sem=send_sem.at[r, k],
                recv_sem=recv_sem.at[r, k],
                device_id={a: to[a]},
                device_id_type=MESH,
            )
            for k, (a, to, src, dst) in enumerate(plans)
        ]

    not_top, not_bottom = gy < sizes["gy"] - 1, gy > 0

    def start_all(r):
        zsend[r, 0] = sz[r, :, :, FIRST, :].astype(BF)
        zsend[r, 1] = sz[r, :, :, FIRST + nz - 1, :].astype(BF)
        both = copies(r)

        @pl.when(not_top)
        def _():
            both[2].start()

        @pl.when(not_bottom)
        def _():
            both[3].start()

        for k in (0, 1, 4, 5):
            both[k].start()
        return both

    def wait_z(r, both):
        both[4].wait_recv()
        both[5].wait_recv()
        sz[r, :, :, FIRST - 1, :] = zrecv[r, 0].astype(F32)
        sz[r, :, :, FIRST + nz, :] = zrecv[r, 1].astype(F32)

    def wait_x(both):
        both[0].wait_recv()
        both[1].wait_recv()

    def wait_y(both):
        @pl.when(not_bottom)
        def _():
            both[2].wait_recv()

        @pl.when(not_top)
        def _():
            both[3].wait_recv()

    def wait_sent(both):
        for k in (0, 1, 4, 5):
            both[k].wait_send()

        @pl.when(not_top)
        def _():
            both[2].wait_send()

        @pl.when(not_bottom)
        def _():
            both[3].wait_send()

    keep_low = jnp.full((nz, h), not_bottom.astype(F32)).astype(BF)
    keep_high = jnp.full((nz, h), not_top.astype(F32)).astype(BF)
    one = jnp.ones((nz, h), BF)

    def block(l, x0, cx, y0, cy):
        for i in range(cx):
            for j in range(cy):
                x, y = x0 + i, y0 + j
                base = selfp[x, y]
                near = (
                    sb[l, x, y + 1],
                    sb[l, x + 2, y + 1],
                    sb[l, x + 1, y],
                    sb[l, x + 1, y + 2],
                    sz[l, x, y, FIRST - 1 : FIRST - 1 + nz, :].astype(BF),
                    sz[l, x, y, FIRST + 1 : FIRST + 1 + nz, :].astype(BF),
                )
                total = None
                for d in range(6):
                    u = (base + bias[l, d]) + near[d]
                    term = u * (one + jnp.tanh(u))
                    if d == 2 and y == 0:
                        term = term * keep_low
                    if d == 3 and y == ny - 1:
                        term = term * keep_high
                    total = term if total is None else total + term
                hs[x, y] = total
        rows = cx * cy * nz
        at = (pl.ds(x0, cx), pl.ds(y0, cy))
        old = lat[at].reshape(rows, h)
        pair = jnp.concatenate([old, hs[at].reshape(rows, h)], axis=1)
        p = jnp.dot(pair, w_pre[l], preferred_element_type=F32).astype(BF)
        inner = p * (jnp.ones_like(p) + jnp.tanh(p))
        update = jnp.dot(inner, w_out[l], preferred_element_type=F32)
        spread = jnp.mean(update * update, axis=1, keepdims=True)
        normed = update * lax.rsqrt(spread + EPSILON) * ngain[l : l + 1, :]
        new = (old.astype(F32) + normed).astype(BF)
        if l == 0:
            lat[at] = new.reshape(cx, cy, nz, h)
            store_parts(1, x0, cx, y0, cy, jnp.dot(new, w_sn[1], preferred_element_type=F32))
        else:
            out_lat[at] = new.reshape(cx, cy, nz, h)
            wide = new.astype(F32).reshape(cx, cy, nz, h)
            for i in range(cx):
                for j in range(cy):
                    flag = flag_t[x0 + i][:, y0 + j : y0 + j + 1]
                    wall[...] += flag * wide[i, j]

    pl.semaphore_wait(barrier, peers)
    for l in range(2):
        both = start_all(l)
        wait_z(l, both)

        @pl.loop(1, nx - 1)
        def _(x):
            block(l, x, 1, 1, ny - 2)

        wait_x(both)

        @pl.loop(0, 2)
        def _(k):
            block(l, k * (nx - 1), 1, 1, ny - 2)

        wait_y(both)
        block(l, 0, nx, 0, 1)
        block(l, 0, nx, ny - 1, 1)
        wait_sent(both)

    red[0, 0, 0:1, :] = jnp.sum(wall[...], axis=0, keepdims=True)
    count = jnp.sum(jnp.sum(jnp.sum(flag_t[...], axis=0), axis=0, keepdims=True), axis=1, keepdims=True)
    red[0, 0, 1:2, :] = jnp.broadcast_to(count, (1, h))
    red[0, 0, 2:8, :] = jnp.zeros((6, h), F32)
    mine = red[0, 0]
    for stage, a in ((0, "gz"), (1, "gy"), (2, "gx")):
        n = sizes[a]
        red[stage + 1, pl.ds(here[a], 1)] = mine[None]
        sent = []
        for k in range(1, n):
            to = lax.rem(here[a] + k, n)
            sent.append(
                pltpu.make_async_remote_copy(
                    src_ref=red.at[stage + 1, here[a]],
                    dst_ref=red.at[stage + 1, here[a]],
                    send_sem=rsend_sem.at[stage, k],
                    recv_sem=rrecv_sem.at[stage, k],
                    device_id={a: to},
                    device_id_type=MESH,
                )
            )
            sent[-1].start()
        for s in sent:
            s.wait()
        mine = red[stage + 1, 0]
        for k in range(1, n):
            mine = mine + red[stage + 1, k]
    out_wall[...] = mine[0:1, :] / mine[1:2, :]


def solution(mesh):
    sizes = {a: mesh.shape[a] for a in AXES}

    def per_device(*args):
        nx, ny, nz, h = dims = args[0].shape
        vmem = pl.BlockSpec(memory_space=pltpu.VMEM)
        latent, mean = pl.pallas_call(
            functools.partial(kernel, sizes, dims),
            out_shape=(
                jax.ShapeDtypeStruct(dims, BF),
                jax.ShapeDtypeStruct((1, h), F32),
            ),
            in_specs=[pl.BlockSpec(memory_space=pl.ANY)] + [vmem] * 13,
            out_specs=(vmem, vmem),
            scratch_shapes=[
                pltpu.VMEM(dims, BF),
                pltpu.VMEM(dims, BF),
                pltpu.VMEM((2, nx + 2, ny + 2, nz, h), BF),
                pltpu.VMEM((2, nx, ny, PITCH, h), F32),
                pltpu.VMEM(dims, BF),
                pltpu.VMEM((nx, nz, ny), F32),
                pltpu.VMEM((2, 2, nx, ny, h), BF),
                pltpu.VMEM((2, 2, nx, ny, h), BF),
                pltpu.VMEM((2, h, 2 * h), BF),
                pltpu.VMEM((2, 2 * h, h), BF),
                pltpu.VMEM((2, h, h), BF),
                pltpu.VMEM((2, 6, nz, h), BF),
                pltpu.VMEM((nz, h), F32),
                pltpu.VMEM((4, 8, 8, h), F32),
                pltpu.SemaphoreType.DMA,
                pltpu.SemaphoreType.DMA,
                pltpu.SemaphoreType.DMA((2, 6)),
                pltpu.SemaphoreType.DMA((2, 6)),
                pltpu.SemaphoreType.DMA((3, 8)),
                pltpu.SemaphoreType.DMA((3, 8)),
            ],
            compiler_params=pltpu.CompilerParams(
                collective_id=0, has_side_effects=True, vmem_limit_bytes=48 * 1024 * 1024
            ),
            name="mesh_step",
        )(*args)
        return latent, mean[0]

    block4 = P(*AXES, None)
    block3 = P(*AXES)
    return jax.shard_map(
        per_device,
        mesh=mesh,
        in_specs=(block4, block3, block3, block3) + (P(),) * 10,
        out_specs=(block4, P()),
        check_vma=False,
    )
```

profile of v0, /device:TPU:1, one launch (start us, length us, event | category | flops | bytes accessed | tf_op | source)
XLA Modules:
  0.0 80.7 jit_solution(3269508356835990373)
XLA Ops:
  0.6 0.7 copy.16.ebias
  1.3 0.0 copy-start
  1.3 1.6 %copy-done = bf16[16,16,32,128]{3,2,1,0:T(8,128)(2,1)S(1)} copy-done((bf16[16,16,32,128]{3,2,1,0:T(8,128)(2,1)S(1)}, bf16[16,16,32,128]{3,2,1,0:T(8,128)(2,1)}, u32[]{:S(2)}) %copy-start) | copy-done | bytes 2097176
  2.9 0.0 copy-start.1
  2.9 0.9 %copy-done.1 = s32[16,16,32]{2,1,0:T(8,128)S(1)} copy-done((s32[16,16,32]{2,1,0:T(8,128)S(1)}, s32[16,16,32]{2,1,0:T(8,128)}, u32[]{:S(2)}) %copy-start.1) | copy-done | bytes 32792
  3.8 0.0 copy-start.2
  3.8 0.9 %copy-done.2 = s32[16,16,32]{2,1,0:T(8,128)S(1)} copy-done((s32[16,16,32]{2,1,0:T(8,128)S(1)}, s32[16,16,32]{2,1,0:T(8,128)}, u32[]{:S(2)}) %copy-start.2) | copy-done | bytes 32792
  4.7 0.0 copy-start.3
  4.7 0.9 %copy-done.3 = s32[16,16,32]{2,1,0:T(8,128)S(1)} copy-done((s32[16,16,32]{2,1,0:T(8,128)S(1)}, s32[16,16,32]{2,1,0:T(8,128)}, u32[]{:S(2)}) %copy-start.3) | copy-done | bytes 32792
  5.6 0.0 copy-start.4
  5.6 0.8 %copy-done.4 = bf16[2,128,128]{2,1,0:T(8,128)(2,1)S(1)} copy-done((bf16[2,128,128]{2,1,0:T(8,128)(2,1)S(1)}, bf16[2,128,128]{2,1,0:T(8,128)(2,1)}, u32[]{:S(2)}) %copy-start.4) | copy-done | bytes 65560
  6.5 0.0 copy-start.5
  6.5 0.8 %copy-done.5 = bf16[2,128,128]{2,1,0:T(8,128)(2,1)S(1)} copy-done((bf16[2,128,128]{2,1,0:T(8,128)(2,1)S(1)}, bf16[2,128,128]{2,1,0:T(8,128)(2,1)}, u32[]{:S(2)}) %copy-start.5) | copy-done | bytes 65560
  7.3 0.0 copy-start.6
  7.3 0.8 %copy-done.6 = bf16[2,128,128]{2,1,0:T(8,128)(2,1)S(1)} copy-done((bf16[2,128,128]{2,1,0:T(8,128)(2,1)S(1)}, bf16[2,128,128]{2,1,0:T(8,128)(2,1)}, u32[]{:S(2)}) %copy-start.6) | copy-done | bytes 65560
  8.1 0.0 copy-start.7
  8.2 0.8 %copy-done.7 = bf16[2,128,128]{2,1,0:T(8,128)(2,1)S(1)} copy-done((bf16[2,128,128]{2,1,0:T(8,128)(2,1)S(1)}, bf16[2,128,128]{2,1,0:T(8,128)(2,1)}, u32[]{:S(2)}) %copy-start.7) | copy-done | bytes 65560
  9.0 0.0 copy-start.8
  9.0 0.8 %copy-done.8 = bf16[2,128,128]{2,1,0:T(8,128)(2,1)S(1)} copy-done((bf16[2,128,128]{2,1,0:T(8,128)(2,1)S(1)}, bf16[2,128,128]{2,1,0:T(8,128)(2,1)}, u32[]{:S(2)}) %copy-start.8) | copy-done | bytes 65560
  9.8 0.0 copy-start.9
  9.8 0.8 %copy-done.9 = bf16[2,128,128]{2,1,0:T(8,128)(2,1)S(1)} copy-done((bf16[2,128,128]{2,1,0:T(8,128)(2,1)S(1)}, bf16[2,128,128]{2,1,0:T(8,128)(2,1)}, u32[]{:S(2)}) %copy-start.9) | copy-done | bytes 65560
  10.7 0.0 copy-start.10
  10.7 0.7 copy-done.10
  11.4 0.0 copy-start.11
  11.4 0.7 copy-done.11
  12.0 0.0 copy-start.12
  12.0 0.7 copy-done.12
  12.7 66.1 %mesh_step.1 = (bf16[16,16,32,128]{3,2,1,0:T(8,128)(2,1)S(1)}, f32[1,128]{1,0:T(1,128)S(1)}) custom-call(bf16[16,16,32,128]{3,2,1,0:T(8,128)(2,1)S(1)} %copy-done, s32[16,16,32]{2,1,0:T(8,128)S(1)} %copy-done.1, s32[16,16,32]{2,1,0:T(8,128)S(1)} %copy-done.2, s32[16,16,32]{2,1,0:T(8,128)S(1)} %copy-done.3, f32[4,128]{1,0:T(4,128)S(1)} %copy-done.10, ...), custom_call_target="tpu_custom_call" | custom-call | tf_op jit(solution)/shard_map/mesh_step/pallas_call | solution.py:309
  78.9 1.3 %copy.19 = bf16[16,16,32,128]{3,2,1,0:T(8,128)(2,1)} copy(bf16[16,16,32,128]{3,2,1,0:T(8,128)(2,1)S(1)} %get-tuple-element.8) | data formatting | bytes 4194304
  80.2 0.5 copy.20
Async XLA Ops:
  1.3 1.6 %copy-start = (bf16[16,16,32,128]{3,2,1,0:T(8,128)(2,1)S(1)}, bf16[16,16,32,128]{3,2,1,0:T(8,128)(2,1)}, u32[]{:S(2)}) copy-start(bf16[16,16,32,128]{3,2,1,0:T(8,128)(2,1)} %feats.1) | copy-start | bytes 6291460
  2.9 0.9 %copy-start.1 = (s32[16,16,32]{2,1,0:T(8,128)S(1)}, s32[16,16,32]{2,1,0:T(8,128)}, u32[]{:S(2)}) copy-start(s32[16,16,32]{2,1,0:T(8,128)} %ntype.1) | copy-start | bytes 98308
  3.8 0.9 %copy-start.2 = (s32[16,16,32]{2,1,0:T(8,128)S(1)}, s32[16,16,32]{2,1,0:T(8,128)}, u32[]{:S(2)}) copy-start(s32[16,16,32]{2,1,0:T(8,128)} %bcode.1) | copy-start | bytes 98308
  4.7 0.9 %copy-start.3 = (s32[16,16,32]{2,1,0:T(8,128)S(1)}, s32[16,16,32]{2,1,0:T(8,128)}, u32[]{:S(2)}) copy-start(s32[16,16,32]{2,1,0:T(8,128)} %wflag.1) | copy-start | bytes 98308
  5.6 0.8 %copy-start.4 = (bf16[2,128,128]{2,1,0:T(8,128)(2,1)S(1)}, bf16[2,128,128]{2,1,0:T(8,128)(2,1)}, u32[]{:S(2)}) copy-start(bf16[2,128,128]{2,1,0:T(8,128)(2,1)} %eself.1) | copy-start | bytes 196612
  6.5 0.8 %copy-start.5 = (bf16[2,128,128]{2,1,0:T(8,128)(2,1)S(1)}, bf16[2,128,128]{2,1,0:T(8,128)(2,1)}, u32[]{:S(2)}) copy-start(bf16[2,128,128]{2,1,0:T(8,128)(2,1)} %enbr.1) | copy-start | bytes 196612
  7.3 0.8 %copy-start.6 = (bf16[2,128,128]{2,1,0:T(8,128)(2,1)S(1)}, bf16[2,128,128]{2,1,0:T(8,128)(2,1)}, u32[]{:S(2)}) copy-start(bf16[2,128,128]{2,1,0:T(8,128)(2,1)} %eout.1) | copy-start | bytes 196612
  8.1 0.8 %copy-start.7 = (bf16[2,128,128]{2,1,0:T(8,128)(2,1)S(1)}, bf16[2,128,128]{2,1,0:T(8,128)(2,1)}, u32[]{:S(2)}) copy-start(bf16[2,128,128]{2,1,0:T(8,128)(2,1)} %nself.1) | copy-start | bytes 196612
  9.0 0.8 %copy-start.8 = (bf16[2,128,128]{2,1,0:T(8,128)(2,1)S(1)}, bf16[2,128,128]{2,1,0:T(8,128)(2,1)}, u32[]{:S(2)}) copy-start(bf16[2,128,128]{2,1,0:T(8,128)(2,1)} %nagg.1) | copy-start | bytes 196612
  9.8 0.8 %copy-start.9 = (bf16[2,128,128]{2,1,0:T(8,128)(2,1)S(1)}, bf16[2,128,128]{2,1,0:T(8,128)(2,1)}, u32[]{:S(2)}) copy-start(bf16[2,128,128]{2,1,0:T(8,128)(2,1)} %nout.1) | copy-start | bytes 196612
  10.7 0.7 copy-start.10
  11.4 0.7 copy-start.11
  12.0 0.7 copy-start.12
where the time goes:
time: 81.2 us; the launch traced here: 80.7 us
  Pallas kernels  66.1 us (81%)
  local copies, waits for them, and re-layouts  13.9 us (17%)
    pallas_call x1, Pallas kernels, per_device(): pl.pallas_call(functools.partial(kernel, sizes, dims), out_shape=(jax.Sha...  66.1 us
    unnamed x29, local copies, waits for them, and re-layouts  13.9 us

commit v1 on v0

v1 whole, which is shorter than its diff:
```python
import functools

import jax
import jax.numpy as jnp
from jax import lax
from jax.experimental import pallas as pl
from jax.experimental.pallas import tpu as pltpu
from jax.sharding import PartitionSpec as P

MESH = pl.DeviceIdType.MESH
AXES = ("gx", "gy", "gz")
EPSILON = 1e-05
BF = jnp.bfloat16
F32 = jnp.float32
PITCH = 48
FIRST = 8
PARTS = 4
CODES = 16


def matmul(a, b):
    return jnp.dot(a, b, preferred_element_type=F32)


def silu_of_double(u):
    return u * (jnp.ones_like(u) + jnp.tanh(u))


def kernel(sizes, dims, *refs):
    hbm, (out_lat, out_wall), vmem, rest = refs[:14], refs[14:16], refs[16:29], refs[29:]
    pl.run_scoped(
        functools.partial(body, sizes, dims, hbm, out_lat, out_wall, vmem, rest),
        *scoped(dims),
    )


def scoped(dims):
    nx, ny, nz, h = dims
    wide = (nx + 2, ny + 2, nz, h)
    return [
        pltpu.VMEM(s, BF)
        for s in (
            dims,
            dims,
            dims,
            wide,
            wide,
            dims,
            dims,
            (2, 2, nx, ny, h),
            (2, 2, nx, ny, h),
            (2, h, 2 * h),
            (2, 2 * h, h),
            (2, h, h),
            (2, 6, nz, h),
            (2 * CODES, 2 * h),
        )
    ]


def body(sizes, dims, hbm, out_lat, out_wall, vmem, rest, *bufs):
    (lat, self0, self1, sb0, sb1, hs, mask, zsend, zrecv, w_sn, w_pre, w_out, bias, tables) = bufs
    (sz0, sz1, flat, wall, line, plane, in_sem, send_sem, recv_sem, rsend_sem, rrecv_sem) = rest
    (ntype, bcode, wflag, ttab, btab, eself, enbr, ebias, eout, nself, nagg, nout, ngain) = vmem
    selfs, sbs, szs = (self0, self1), (sb0, sb1), (sz0, sz1)
    nx, ny, nz, h = dims
    here = {a: lax.axis_index(a) for a in AXES}
    gy = here["gy"]
    not_top, not_bottom = gy < sizes["gy"] - 1, gy > 0

    loads = [
        pltpu.make_async_copy(src, dst, in_sem.at[k])
        for k, (src, dst) in enumerate(zip(hbm, (lat,) + vmem, strict=True))
    ]
    for k in (1, 2, 3, 4, 5, 0, 6, 7, 8, 9, 10, 11, 12, 13):
        loads[k].start()

    barrier = pltpu.get_barrier_semaphore()
    planes = sizes["gx"] * sizes["gy"]
    peers = [{"gz": lax.rem(here["gz"] + k, sizes["gz"])} for k in range(1, sizes["gz"])]
    for k in range(1, planes):
        j = lax.rem(here["gx"] * sizes["gy"] + here["gy"] + k, planes)
        peers.append({"gx": lax.div(j, sizes["gy"]), "gy": lax.rem(j, sizes["gy"])})
    for peer in peers:
        pl.semaphore_signal(barrier, inc=1, device_id=peer, device_id_type=MESH)

    wall[...] = jnp.zeros_like(wall)

    def exchange(slots, spot, n, place, stage):
        sent = []
        for k in range(1, n):
            sent.append(
                pltpu.make_async_remote_copy(
                    src_ref=slots.at[spot],
                    dst_ref=slots.at[spot],
                    send_sem=rsend_sem.at[stage, k],
                    recv_sem=rrecv_sem.at[stage, k],
                    device_id=place(lax.rem(spot + k, n)),
                    device_id_type=MESH,
                )
            )
            sent[-1].start()
        return sent

    def total_of(sent, slots, n):
        for s in sent:
            s.wait()
        total = slots[0]
        for k in range(1, n):
            total = total + slots[k]
        return total

    @pl.when(gy == 0)
    def _():
        @pl.loop(1, nx + 1)
        def _(x):
            sb0[x, 0] = jnp.zeros((nz, h), BF)
            sb1[x, 0] = jnp.zeros((nz, h), BF)

    @pl.when(gy == sizes["gy"] - 1)
    def _():
        @pl.loop(1, nx + 1)
        def _(x):
            sb0[x, ny + 1] = jnp.zeros((nz, h), BF)
            sb1[x, ny + 1] = jnp.zeros((nz, h), BF)

    for k in range(1, 6):
        loads[k].wait()

    columns, per_row = nx * ny, h // nz
    code = (ntype[...] + 4 * bcode[...] + CODES * wflag[...]).astype(F32)
    code = code.reshape(columns, nz).astype(BF)
    iota = lambda shape, d: lax.broadcasted_iota(jnp.int32, shape, d)
    ones_where = lambda hit: jnp.where(hit, 1.0, 0.0)
    repeat = ones_where(lax.rem(iota((nz, h), 1), nz) == iota((nz, h), 0)).astype(BF)
    spread_out = matmul(code, repeat)
    mine = lax.rem(iota((columns, h), 0), per_row) == lax.div(iota((columns, h), 1), nz)
    spread_out = jnp.where(mine, spread_out, 0.0).astype(BF)
    blocks = columns // per_row
    gather = ones_where(
        lax.div(iota((blocks, columns), 1), per_row) == iota((blocks, columns), 0)
    ).astype(BF)
    flat[...] = matmul(gather, spread_out)
    flags = ones_where(flat[...] >= CODES)
    count = jnp.sum(jnp.sum(flags, axis=0, keepdims=True), axis=1, keepdims=True)
    line[pl.ds(here["gz"], 1), 1:2, :] = jnp.broadcast_to(count, (1, h))[None]

    sums = jnp.concatenate(
        [ttab[...] + btab[b : b + 1, :] for b in range(3)] + [jnp.zeros((4, h), F32)], axis=0
    )
    high = sums.astype(BF)
    low = (sums - high.astype(F32)).astype(BF)
    tables[0:CODES, :h] = high
    tables[CODES : 2 * CODES, :h] = low
    last = iota((2 * CODES, h), 0) == 2 * CODES - 1
    tables[:, h:] = ones_where(last).astype(BF)

    for k in range(6, 14):
        loads[k].wait()
    for l in range(2):
        w_sn[l, :, :h] = (eself[l].astype(F32) * 0.5).astype(BF)
        w_sn[l, :, h:] = (enbr[l].astype(F32) * 0.5).astype(BF)
        w_pre[l, :h, :] = (nself[l].astype(F32) * 0.5).astype(BF)
        w_pre[l, h:, :] = (matmul(eout[l], nagg[l]) * 0.5).astype(BF)
        w = nout[l].astype(F32)
        w_out[l] = (w - jnp.mean(w, axis=1, keepdims=True)).astype(BF)
        for d in range(6):
            row = ebias[d, l : l + 1, :] * 0.5
            bias[l, d] = jnp.broadcast_to(row, (nz, h)).astype(BF)

    loads[0].wait()
    per_x = ny // per_row

    def begin(x):
        nodes = ny * nz
        rows = [flat[pl.ds(x * per_x + k, 1), :] for k in range(per_x)]
        nodes_code = jnp.broadcast_to(jnp.concatenate(rows, axis=1), (2 * CODES, nodes))
        on_wall = nodes_code >= CODES
        kind = jnp.where(on_wall, nodes_code - CODES, nodes_code)
        at = iota((2 * CODES, nodes), 0)
        hit = kind == lax.rem(at, CODES).astype(F32)
        hot = jnp.where(at == 2 * CODES - 1, ones_where(on_wall), ones_where(hit)).astype(BF)
        found = lax.dot_general(
            hot, tables[...], (((0,), (0,)), ((), ())), preferred_element_type=F32
        )
        new = (lat[x].reshape(nodes, h).astype(F32) + found[:, :h]).astype(BF)
        return new, found[:, h:].astype(BF), matmul(new, w_sn[0])

    def store_parts(r, at, shape, both):
        x, y = at
        s = both[:, h:].reshape(shape)
        selfs[r][x, y] = both[:, :h].astype(BF).reshape(shape)
        sbs[r][shift(x), shift(y)] = s.astype(BF)
        szs[r][x, y, FIRST : FIRST + nz, :] = s

    def shift(i):
        return pl.ds(i.start + 1, i.size) if isinstance(i, pl.Slice) else i + 1

    with jax.named_scope("prologue"):

        @pl.loop(0, nx // 2)
        def _(i):
            xs = (2 * i, 2 * i + 1)
            results = [begin(x) for x in xs]
            for x, (new, walls, both) in zip(xs, results, strict=True):
                lat[x] = new.reshape(ny, nz, h)
                mask[x] = walls.reshape(ny, nz, h)
                store_parts(0, (x, pl.ds(0, ny)), (ny, nz, h), both)

    def copies(r):
        up = {a: lax.rem(here[a] + 1, sizes[a]) for a in AXES}
        down = {a: lax.rem(here[a] + sizes[a] - 1, sizes[a]) for a in AXES}
        sb = sbs[r]
        rows_x, rows_y = pl.ds(1, nx), pl.ds(1, ny)
        plans = (
            ("gx", up, sb.at[nx, rows_y], sb.at[0, rows_y]),
            ("gx", down, sb.at[1, rows_y], sb.at[nx + 1, rows_y]),
            ("gy", up, sb.at[rows_x, ny], sb.at[rows_x, 0]),
            ("gy", down, sb.at[rows_x, 1], sb.at[rows_x, ny + 1]),
            ("gz", up, zsend.at[r, 1], zrecv.at[r, 0]),
            ("gz", down, zsend.at[r, 0], zrecv.at[r, 1]),
        )
        return [
            pltpu.make_async_remote_copy(
                src_ref=src,
                dst_ref=dst,
                send_sem=send_sem.at[r, k],
                recv_sem=recv_sem.at[r, k],
                device_id={a: to[a]},
                device_id_type=MESH,
            )
            for k, (a, to, src, dst) in enumerate(plans)
        ]

    def start_all(r):
        both = copies(r)
        for k in (0, 1):
            both[k].start()

        @pl.when(not_top)
        def _():
            both[2].start()

        @pl.when(not_bottom)
        def _():
            both[3].start()

        zsend[r, 0] = szs[r][:, :, FIRST, :].astype(BF)
        zsend[r, 1] = szs[r][:, :, FIRST + nz - 1, :].astype(BF)
        for k in (4, 5):
            both[k].start()
        return both

    def wait_z(r, both):
        both[4].wait_recv()
        both[5].wait_recv()
        szs[r][:, :, FIRST - 1, :] = zrecv[r, 0].astype(F32)
        szs[r][:, :, FIRST + nz, :] = zrecv[r, 1].astype(F32)

    def wait_x(both):
        both[0].wait_recv()
        both[1].wait_recv()

    def wait_y(both):
        @pl.when(not_bottom)
        def _():
            both[2].wait_recv()

        @pl.when(not_top)
        def _():
            both[3].wait_recv()

    def wait_sent(both):
        for k in (0, 1, 4, 5):
            both[k].wait_send()

        @pl.when(not_top)
        def _():
            both[2].wait_send()

        @pl.when(not_bottom)
        def _():
            both[3].wait_send()

    def edges(l, x, y, dirs, total):
        base = selfs[l][x, y]
        for d in dirs:
            if d < 4:
                near = sbs[l][x + (0, 2, 1, 1)[d], y + (1, 1, 0, 2)[d]]
            else:
                first = FIRST + (-1, 1)[d - 4]
                near = szs[l][x, y, first : first + nz, :].astype(BF)
            term = silu_of_double((base + bias[l, d]) + near)
            if d == 2 and y == 0:
                term = term * keep(not_bottom)
            if d == 3 and y == ny - 1:
                term = term * keep(not_top)
            total = term if total is None else total + term
        return total

    def keep(cond):
        return jnp.full((nz, h), cond.astype(F32)).astype(BF)

    inner_y = range(1, ny - 1)

    def edges_xy(l, x):
        for y in inner_y:
            hs[x, y] = edges(l, x, y, (0, 1, 2, 3), None)

    def edges_z(l, xs):
        sums = [(x, y, edges(l, x, y, (4, 5), hs[x, y])) for x in xs for y in inner_y]
        for x, y, total in sums:
            hs[x, y] = total

    def node(l, ats, shape):
        rows = 1
        for s in shape[:-1]:
            rows *= s
        take = lambda ref: jnp.concatenate([ref[at].reshape(rows, h) for at in ats], axis=0)
        old = take(lat)
        p = matmul(jnp.concatenate([old, take(hs)], axis=1), w_pre[l]).astype(BF)
        update = matmul(silu_of_double(p), w_out[l])
        spread = jnp.mean(update * update, axis=1, keepdims=True)
        normed = update * lax.rsqrt(spread + EPSILON) * ngain[l : l + 1, :]
        new = (old.astype(F32) + normed).astype(BF)
        part = lambda v, k: v[k * rows : (k + 1) * rows]
        if l == 0:
            both = matmul(new, w_sn[1])
            for k, at in enumerate(ats):
                lat[at] = part(new, k).reshape(shape)
                store_parts(1, at, shape, part(both, k))
        else:
            on_wall = (new * take(mask)).astype(F32)
            wall[...] += jnp.sum(on_wall.reshape(-1, 8, h), axis=0)
            for k, at in enumerate(ats):
                lat[at] = part(new, k).reshape(shape)

    def pair(i):
        face = i == nx // 2 - 1
        return jnp.where(face, 0, 2 * i + 1), jnp.where(face, nx - 1, 2 * i + 2)

    def node_pair(l, i):
        node(l, [(x, pl.ds(1, ny - 2)) for x in pair(i)], (ny - 2, nz, h))

    with jax.named_scope("bar"):
        pl.semaphore_wait(barrier, len(peers))
    for l in range(2):
        with jax.named_scope(f"start{l}"):
            both = start_all(l)
        with jax.named_scope(f"pre{l}"):

            @pl.loop(1, nx - 1)
            def _(x):
                edges_xy(l, x)

        with jax.named_scope(f"waitz{l}"):
            wait_z(l, both)
        with jax.named_scope(f"main{l}"):
            edges_z(l, pair(0))

            @pl.loop(1, nx // 2)
            def _(i):
                @pl.when(i == nx // 2 - 1)
                def _():
                    with jax.named_scope(f"waitx{l}"):
                        wait_x(both)

                    @pl.loop(0, 2)
                    def _(k):
                        edges_xy(l, k * (nx - 1))

                node_pair(l, i - 1)
                edges_z(l, pair(i))

        with jax.named_scope(f"waity{l}"):
            wait_y(both)
        with jax.named_scope(f"by{l}"):
            node_pair(l, nx // 2 - 1)
            for y in (0, ny - 1):

                @pl.loop(0, nx, unroll=4)
                def _(x):
                    hs[x, y] = edges(l, x, y, range(6), None)

            node(l, [(pl.ds(0, nx), 0), (pl.ds(0, nx), ny - 1)], (nx, nz, h))
        with jax.named_scope(f"waits{l}"):
            wait_sent(both)

    leave = pltpu.make_async_copy(lat, out_lat, in_sem.at[0])
    leave.start()
    with jax.named_scope("allred"):
        line[pl.ds(here["gz"], 1), 0:1, :] = jnp.sum(wall[...], axis=0, keepdims=True)[None]
        sent = exchange(line, here["gz"], sizes["gz"], lambda j: {"gz": j}, 0)
        total = total_of(sent, line, sizes["gz"])
        spot = here["gx"] * sizes["gy"] + here["gy"]
        plane[pl.ds(spot, 1)] = total[None]
        place = lambda j: {"gx": lax.div(j, sizes["gy"]), "gy": lax.rem(j, sizes["gy"])}
        sent = exchange(plane, spot, sizes["gx"] * sizes["gy"], place, 1)
        total = total_of(sent, plane, sizes["gx"] * sizes["gy"])
        out_wall[...] = total[0:1, :] / total[1:2, :]
    leave.wait()


def hand_over(latent, mean, out_latent, out_mean, held, held_mean, in_sem, out_sem):
    step = latent.shape[0] // PARTS
    parts = [pl.ds(k * step, step) for k in range(PARTS)]
    ways = [(latent.at[p], held.at[p], out_latent.at[p]) for p in parts]
    ways.append((mean, held_mean, out_mean))
    comes = [pltpu.make_async_copy(w[0], w[1], in_sem.at[k]) for k, w in enumerate(ways)]
    goes = [pltpu.make_async_copy(w[1], w[2], out_sem.at[k]) for k, w in enumerate(ways)]
    for c in comes:
        c.start()
    for c, g in zip(comes, goes, strict=True):
        c.wait()
        g.start()
    for g in goes:
        g.wait()


def solution(mesh):
    sizes = {a: mesh.shape[a] for a in AXES}

    def per_device(*args):
        args = list(args)
        args[8] = jnp.transpose(args[8], (1, 0, 2))
        nx, ny, nz, h = dims = args[0].shape
        hbm = pl.BlockSpec(memory_space=pltpu.HBM)
        vmem = pl.BlockSpec(memory_space=pltpu.VMEM)
        latent, mean = pl.pallas_call(
            functools.partial(kernel, sizes, dims),
            out_shape=(
                jax.ShapeDtypeStruct(dims, BF),
                jax.ShapeDtypeStruct((1, h), F32),
            ),
            in_specs=[hbm] * 14,
            out_specs=(hbm, vmem),
            scratch_shapes=[pltpu.VMEM(a.shape, a.dtype) for a in args[1:]]
            + [
                pltpu.VMEM((nx, ny, PITCH, h), F32),
                pltpu.VMEM((nx, ny, PITCH, h), F32),
                pltpu.VMEM((nx * ny * nz // h, h), F32),
                pltpu.VMEM((8, h), F32),
                pltpu.VMEM((sizes["gz"], 2, h), F32),
                pltpu.VMEM((sizes["gx"] * sizes["gy"], 2, h), F32),
                pltpu.SemaphoreType.DMA((14,)),
                pltpu.SemaphoreType.DMA((2, 6)),
                pltpu.SemaphoreType.DMA((2, 6)),
                pltpu.SemaphoreType.DMA((2, 32)),
                pltpu.SemaphoreType.DMA((2, 32)),
            ],
            compiler_params=pltpu.CompilerParams(
                collective_id=0, has_side_effects=True, vmem_limit_bytes=58 * 1024 * 1024
            ),
            name="mesh_step",
        )(*args)
        latent, mean = pl.pallas_call(
            hand_over,
            out_shape=(
                jax.ShapeDtypeStruct(dims, BF),
                jax.ShapeDtypeStruct((1, h), F32),
            ),
            in_specs=[hbm, hbm],
            out_specs=(hbm, hbm),
            scratch_shapes=[
                pltpu.VMEM(dims, BF),
                pltpu.VMEM((1, h), F32),
                pltpu.SemaphoreType.DMA((PARTS + 1,)),
                pltpu.SemaphoreType.DMA((PARTS + 1,)),
            ],
            compiler_params=pltpu.CompilerParams(vmem_limit_bytes=58 * 1024 * 1024),
            name="hand_over",
        )(latent, mean)
        return latent, mean[0]

    block4 = P(*AXES, None)
    block3 = P(*AXES)
    return jax.shard_map(
        per_device,
        mesh=mesh,
        in_specs=(block4, block3, block3, block3) + (P(),) * 10,
        out_specs=(block4, P()),
        check_vma=False,
    )
```

time: 81.2 us -> 53.5 us (0.66)
  local copies, waits for them, and re-layouts: 13.9 us -> 0 us
  Pallas kernels: 66.1 us -> 52.7 us
    pallas_call x1, Pallas kernels: 66.1 us -> 50.3 us  [per_device(): pl.pallas_call(functools.partial(kernel, sizes, dims), out_shape=(jax.Sha...]
    unnamed x29 -> x0, local copies, waits for them, and re-layouts: 13.9 us -> none
    pallas_call x0 -> x1, Pallas kernels: none -> 2.44 us  [per_device(): pl.pallas_call(hand_over, out_shape=(jax.ShapeDtypeStruct(dims, BF), jax....]
where the time goes in v1:
time: 53.5 us; the launch traced here: 53.4 us
  Pallas kernels  52.7 us (99%)
  between operations  0.64 us (1%)
    pallas_call x1, Pallas kernels, per_device(): pl.pallas_call(functools.partial(kernel, sizes, dims), out_shape=(jax.Sha...  50.3 us
    pallas_call x1, Pallas kernels, per_device(): pl.pallas_call(hand_over, out_shape=(jax.ShapeDtypeStruct(dims, BF), jax....  2.44 us

profile of v1, /device:TPU:1, one launch (start us, length us, event | category | flops | bytes accessed | tf_op | source)
XLA Modules:
  0.0 53.4 jit_solution(2041947455649900513)
XLA Ops:
  0.6 50.3 %mesh_step.1 = (bf16[16,16,32,128]{3,2,1,0:T(8,128)(2,1)}, f32[1,128]{1,0:T(1,128)}) custom-call(bf16[16,16,32,128]{3,2,1,0:T(8,128)(2,1)} %refs_0_.1, s32[16,16,32]{2,1,0:T(8,128)} %refs_1_.1, s32[16,16,32]{2,1,0:T(8,128)} %refs_2_.1, s32[16,16,32]{2,1,0:T(8,128)} %refs_3_.1, f32[4,128]{1,0:T(4,128)} %refs_4_.1, f32[3,128]{1,0:T(4,128)} %refs_5_.1, ...), custom_call_target="tpu_custom_call" | custom-call | tf_op jit(solution)/shard_map/mesh_step/pallas_call | solution.py:429
  51.0 2.4 %hand_over.1 = (bf16[16,16,32,128]{3,2,1,0:T(8,128)(2,1)}, f32[1,128]{1,0:T(1,128)}) custom-call(bf16[16,16,32,128]{3,2,1,0:T(8,128)(2,1)} %get-tuple-element.6.latent, f32[1,128]{1,0:T(1,128)} %get-tuple-element.7.mean), custom_call_target="tpu_custom_call" | custom-call | tf_op jit(solution)/shard_map/hand_over/pallas_call | solution.py:456

commit v2 on v1

v2 whole, which is shorter than its diff:
```python
import functools

import jax
import jax.numpy as jnp
from jax import lax
from jax.experimental import pallas as pl
from jax.experimental.pallas import tpu as pltpu
from jax.sharding import PartitionSpec as P

MESH = pl.DeviceIdType.MESH
AXES = ("gx", "gy", "gz")
EPSILON = 1e-05
BF = jnp.bfloat16
F32 = jnp.float32
PITCH = 48
FIRST = 8
PARTS = 4
SPARE = 3
CODES = 16


def matmul(a, b):
    return jnp.dot(a, b, preferred_element_type=F32)


def silu_of_double(u):
    return u * (jnp.ones_like(u) + jnp.tanh(u))


def kernel(sizes, dims, *refs):
    hbm, (out_lat, out_wall), vmem, rest = refs[:14], refs[14:16], refs[16:29], refs[29:]
    pl.run_scoped(
        functools.partial(body, sizes, dims, hbm, out_lat, out_wall, vmem, rest),
        *scoped(dims),
    )


def scoped(dims):
    nx, ny, nz, h = dims
    more = (nx + SPARE, ny, nz, h)
    wide = (nx + SPARE + 1, ny + 2, nz, h)
    return [
        pltpu.VMEM(s, BF)
        for s in (
            more,
            more,
            more,
            wide,
            wide,
            more,
            more,
            (2, 2, nx, ny, h),
            (2, 2, nx, ny, h),
            (2, h, 2 * h),
            (2, 2 * h, h),
            (2, h, h),
            (2, 6, nz, h),
            (2 * CODES, 2 * h),
        )
    ]


def body(sizes, dims, hbm, out_lat, out_wall, vmem, rest, *bufs):
    (lat, self0, self1, sb0, sb1, hs, mask, zsend, zrecv, w_sn, w_pre, w_out, bias, tables) = bufs
    (sz0, sz1, flat, upd, wall, line, plane, in_sem, send_sem, recv_sem, rsend_sem, rrecv_sem) = rest
    (ntype, bcode, wflag, ttab, btab, eself, enbr, ebias, eout, nself, nagg, nout, ngain) = vmem
    selfs, sbs, szs = (self0, self1), (sb0, sb1), (sz0, sz1)
    nx, ny, nz, h = dims
    here = {a: lax.axis_index(a) for a in AXES}
    gy = here["gy"]
    not_top, not_bottom = gy < sizes["gy"] - 1, gy > 0

    loads = [
        pltpu.make_async_copy(src, dst, in_sem.at[k])
        for k, (src, dst) in enumerate(zip(hbm, (lat.at[pl.ds(0, nx)],) + vmem, strict=True))
    ]
    for k in (1, 2, 3, 0, 4, 5, 6, 7, 8, 9, 10, 11, 12, 13):
        loads[k].start()

    barrier = pltpu.get_barrier_semaphore()
    planes = sizes["gx"] * sizes["gy"]
    peers = [{"gz": lax.rem(here["gz"] + k, sizes["gz"])} for k in range(1, sizes["gz"])]
    for k in range(1, planes):
        j = lax.rem(here["gx"] * sizes["gy"] + here["gy"] + k, planes)
        peers.append({"gx": lax.div(j, sizes["gy"]), "gy": lax.rem(j, sizes["gy"])})
    for peer in peers:
        pl.semaphore_signal(barrier, inc=1, device_id=peer, device_id_type=MESH)

    wall[...] = jnp.zeros_like(wall)

    def exchange(slots, spot, n, place, stage):
        def copy(ref, to):
            return pltpu.make_async_remote_copy(
                src_ref=ref,
                dst_ref=ref,
                send_sem=rsend_sem.at[stage],
                recv_sem=rrecv_sem.at[stage],
                device_id=place(to),
                device_id_type=MESH,
            )

        for k in range(1, n):
            copy(slots.at[spot], lax.rem(spot + k, n)).start()
        copy(slots.at[pl.ds(0, n - 1)], lax.rem(spot + 1, n)).wait()
        total = slots[0]
        for k in range(1, n):
            total = total + slots[k]
        return total

    upd[...] = jnp.zeros_like(upd)
    spare = (nx + 1, nx + 2)
    for x in spare:
        for ref in (lat, hs, mask):
            ref[x] = jnp.zeros((ny, nz, h), BF)

    @pl.when(gy == 0)
    def _():
        @pl.loop(1, nx + 1)
        def _(x):
            sb0[x, 0] = jnp.zeros((nz, h), BF)
            sb1[x, 0] = jnp.zeros((nz, h), BF)

    @pl.when(gy == sizes["gy"] - 1)
    def _():
        @pl.loop(1, nx + 1)
        def _(x):
            sb0[x, ny + 1] = jnp.zeros((nz, h), BF)
            sb1[x, ny + 1] = jnp.zeros((nz, h), BF)

    for k in range(1, 6):
        loads[k].wait()

    columns, per_row = nx * ny, h // nz
    code = (ntype[...] + 4 * bcode[...] + CODES * wflag[...]).astype(F32)
    code = code.reshape(columns, nz).astype(BF)
    iota = lambda shape, d: lax.broadcasted_iota(jnp.int32, shape, d)
    ones_where = lambda hit: jnp.where(hit, 1.0, 0.0)
    repeat = ones_where(lax.rem(iota((nz, h), 1), nz) == iota((nz, h), 0)).astype(BF)
    spread_out = matmul(code, repeat)
    turned = lambda y: lax.rem(y + 1, ny)
    slot = lax.rem(turned(lax.rem(iota((columns, h), 0), ny)), per_row)
    spread_out = jnp.where(slot == lax.div(iota((columns, h), 1), nz), spread_out, 0.0).astype(BF)
    per_x = ny // per_row
    blocks = (nx * per_x, columns)
    row, column = iota(blocks, 0), iota(blocks, 1)
    belongs = jnp.logical_and(
        lax.rem(row, nx) == lax.div(column, ny),
        lax.div(row, nx) == lax.div(turned(lax.rem(column, ny)), per_row),
    )
    flat[...] = matmul(ones_where(belongs).astype(BF), spread_out)

    sums = jnp.concatenate(
        [ttab[...] + btab[b : b + 1, :] for b in range(3)] + [jnp.zeros((4, h), F32)], axis=0
    )
    high = sums.astype(BF)
    low = (sums - high.astype(F32)).astype(BF)
    tables[0:CODES, :h] = high
    tables[CODES : 2 * CODES, :h] = low
    last = iota((2 * CODES, h), 0) == 2 * CODES - 1
    tables[:, h:] = ones_where(last).astype(BF)

    def prepare(l):
        w_pre[l, :h, :] = (nself[l].astype(F32) * 0.5).astype(BF)
        w_pre[l, h:, :] = (matmul(eout[l], nagg[l]) * 0.5).astype(BF)
        w = nout[l].astype(F32)
        w_out[l] = (w - jnp.mean(w, axis=1, keepdims=True)).astype(BF)
        for d in range(6):
            row = ebias[d, l : l + 1, :] * 0.5
            bias[l, d] = jnp.broadcast_to(row, (nz, h)).astype(BF)

    for k in range(6, 14):
        loads[k].wait()
    for l in range(2):
        w_sn[l, :, :h] = (eself[l].astype(F32) * 0.5).astype(BF)
        w_sn[l, :, h:] = (enbr[l].astype(F32) * 0.5).astype(BF)
    loads[0].wait()

    for k, z in enumerate((0, nz - 1)):
        kind = jnp.broadcast_to(code[:, z : z + 1].astype(F32), (columns, 2 * CODES))
        kind = jnp.where(kind >= CODES, kind - CODES, kind)
        hot = ones_where(kind == lax.rem(iota((columns, 2 * CODES), 1), CODES).astype(F32))
        found = matmul(hot.astype(BF), tables[:, :h])
        face = lat[0:nx, :, z, :].astype(F32).reshape(columns, h)
        new = (face + found).astype(BF)
        zsend[0, k] = matmul(new, w_sn[0, :, h:]).astype(BF).reshape(nx, ny, h)

    def begin(rows, ats, shapes):
        nodes = len(rows) * h
        nodes_code = jnp.concatenate([flat[pl.ds(r, 1), :] for r in rows], axis=1)
        nodes_code = jnp.broadcast_to(nodes_code, (2 * CODES, nodes))
        on_wall = nodes_code >= CODES
        kind = jnp.where(on_wall, nodes_code - CODES, nodes_code)
        at = iota((2 * CODES, nodes), 0)
        hit = kind == lax.rem(at, CODES).astype(F32)
        hot = jnp.where(at == 2 * CODES - 1, ones_where(on_wall), ones_where(hit)).astype(BF)
        found = lax.dot_general(
            hot, tables[...], (((0,), (0,)), ((), ())), preferred_element_type=F32
        )
        old = jnp.concatenate([lat[at].reshape(-1, h) for at in ats], axis=0)
        new = (old.astype(F32) + found[:, :h]).astype(BF)
        walls = found[:, h:].astype(BF)
        both = matmul(new, w_sn[0])
        first = 0
        for at, shape in zip(ats, shapes, strict=True):
            part = slice(first, first + shape[0] * nz)
            first += shape[0] * nz
            lat[at] = new[part].reshape(shape)
            mask[at] = walls[part].reshape(shape)
            store_parts(0, at, shape, both[part])

    def store_parts(r, at, shape, both):
        x, y = at
        s = both[:, h:].reshape(shape)
        selfs[r][x, y] = both[:, :h].astype(BF).reshape(shape)
        sbs[r][shift(x), shift(y)] = s.astype(BF)
        szs[r][x, y, FIRST : FIRST + nz, :] = s

    def shift(i):
        return pl.ds(i.start + 1, i.size) if isinstance(i, pl.Slice) else i + 1

    def copies(r):
        up = {a: lax.rem(here[a] + 1, sizes[a]) for a in AXES}
        down = {a: lax.rem(here[a] + sizes[a] - 1, sizes[a]) for a in AXES}
        sb = sbs[r]
        rows_x, rows_y = pl.ds(1, nx), pl.ds(1, ny)
        plans = (
            ("gx", up, sb.at[nx, rows_y], sb.at[0, rows_y]),
            ("gx", down, sb.at[1, rows_y], sb.at[nx + 1, rows_y]),
            ("gy", up, sb.at[rows_x, ny], sb.at[rows_x, 0]),
            ("gy", down, sb.at[rows_x, 1], sb.at[rows_x, ny + 1]),
            ("gz", up, zsend.at[r, 1], zrecv.at[r, 0]),
            ("gz", down, zsend.at[r, 0], zrecv.at[r, 1]),
        )
        return [
            pltpu.make_async_remote_copy(
                src_ref=src,
                dst_ref=dst,
                send_sem=send_sem.at[r, k],
                recv_sem=recv_sem.at[r, k],
                device_id={a: to[a]},
                device_id_type=MESH,
            )
            for k, (a, to, src, dst) in enumerate(plans)
        ]

    def start_z(both):
        both[4].start()
        both[5].start()

    def start_x(both):
        both[0].start()
        both[1].start()

    def start_y(both):
        @pl.when(not_top)
        def _():
            both[2].start()

        @pl.when(not_bottom)
        def _():
            both[3].start()

    def wait_z(r, both):
        both[4].wait_recv()
        both[5].wait_recv()
        szs[r][0:nx, :, FIRST - 1, :] = zrecv[r, 0].astype(F32)
        szs[r][0:nx, :, FIRST + nz, :] = zrecv[r, 1].astype(F32)

    def wait_x(both):
        both[0].wait_recv()
        both[1].wait_recv()

    def wait_y(both):
        @pl.when(not_bottom)
        def _():
            both[2].wait_recv()

        @pl.when(not_top)
        def _():
            both[3].wait_recv()

    def wait_sent(both):
        for k in (0, 1, 4, 5):
            both[k].wait_send()

        @pl.when(not_top)
        def _():
            both[2].wait_send()

        @pl.when(not_bottom)
        def _():
            both[3].wait_send()

    def edges(l, x, y, dirs, total):
        base = selfs[l][x, y]
        for d in dirs:
            if d < 4:
                near = sbs[l][x + (0, 2, 1, 1)[d], y + (1, 1, 0, 2)[d]]
            else:
                first = FIRST + (-1, 1)[d - 4]
                near = szs[l][x, y, first : first + nz, :].astype(BF)
            term = silu_of_double((base + bias[l, d]) + near)
            if d == 2 and y == 0:
                term = term * keep(not_bottom)
            if d == 3 and y == ny - 1:
                term = term * keep(not_top)
            total = term if total is None else total + term
        return total

    def keep(cond):
        return jnp.full((nz, h), cond.astype(F32)).astype(BF)

    def take(ref, ats):
        return jnp.concatenate([ref[at].reshape(-1, h) for at in ats], axis=0)

    def update_of(l, old, hidden):
        p = matmul(jnp.concatenate([old, hidden], axis=1), w_pre[l]).astype(BF)
        return matmul(silu_of_double(p), w_out[l])

    def latent_of(l, old, update):
        spread = jnp.mean(update * update, axis=1, keepdims=True)
        normed = update * lax.rsqrt(spread + EPSILON) * ngain[l : l + 1, :]
        return (old.astype(F32) + normed).astype(BF)

    def finish(l, ats, shape, new, walls):
        rows = new.shape[0] // len(ats)
        both = matmul(new, w_sn[1]) if l == 0 else None
        if l == 1:
            wall[...] += jnp.sum((new * walls).astype(F32).reshape(-1, 8, h), axis=0)
        for k, at in enumerate(ats):
            part = slice(k * rows, (k + 1) * rows)
            if l == 0:
                lat[at] = new[part].reshape(shape)
                store_parts(1, at, shape, both[part])
            else:
                out_lat[at] = new[part].reshape(shape)

    face = nx // 2 - 1

    def pair(i):
        if isinstance(i, int):
            return (0, nx - 1) if i == face else (2 * i + 1, 2 * i + 2)
        first = jnp.where(i == face, 0, 2 * i + 1)
        second = jnp.where(i == face, nx - 1, 2 * i + 2)
        return jnp.where(i < 0, spare[0], first), jnp.where(i < 0, spare[1], second)

    inner = pl.ds(1, ny - 2)
    inner_shape = (ny - 2, nz, h)
    inner_rows = 2 * (ny - 2) * nz
    ats_of = lambda i: [(x, inner) for x in pair(i)]
    walls_of = lambda l, ats: take(mask, ats) if l == 1 else None
    y_ats = [(pl.ds(0, nx), 0), (pl.ds(0, nx), ny - 1)]

    travel = [copies(0), copies(1)]
    with jax.named_scope("prologue"):

        @pl.loop(0, 2)
        def _(c):
            half = nx // 2
            xs = [half * c + k for k in range(half)]
            ats, shapes = [], []
            for x in xs:
                ats += [(x, pl.ds(ny - 1, 1)), (x, pl.ds(0, per_row - 1))]
                shapes += [(1, nz, h), (per_row - 1, nz, h)]
            begin(xs, ats, shapes)

        with jax.named_scope("bar"):
            pl.semaphore_wait(barrier, len(peers))
        start_z(travel[0])
        start_y(travel[0])

        @pl.loop(0, nx // 2)
        def _(i):
            xs = (jnp.where(i == 0, 0, 2 * i - 1), jnp.where(i == 0, nx - 1, 2 * i))
            rest = ny - per_row
            rows = [g * nx + x for x in xs for g in range(1, per_x)]
            begin(rows, [(x, pl.ds(per_row - 1, rest)) for x in xs], [(rest, nz, h)] * 2)

            @pl.when(i == 0)
            def _():
                start_x(travel[0])

        prepare(0)

    for l in range(2):
        both = travel[l]
        if l == 1:
            with jax.named_scope("start1"):
                start_y(both)
                start_x(both)
                zsend[1, 0] = sz1[0:nx, :, FIRST, :].astype(BF)
                zsend[1, 1] = sz1[0:nx, :, FIRST + nz - 1, :].astype(BF)
                start_z(both)
                prepare(1)
                flags = ones_where(flat[...] >= CODES)
                count = jnp.sum(jnp.sum(flags, axis=0, keepdims=True), axis=1, keepdims=True)
                line[pl.ds(here["gz"], 1), 1:2, :] = jnp.broadcast_to(count, (1, h))[None]
        with jax.named_scope(f"waitz{l}"):
            wait_z(l, both)
        with jax.named_scope(f"main{l}"):

            @pl.loop(0, nx // 2)
            def _(i):
                @pl.when(i == face)
                def _():
                    with jax.named_scope(f"waitx{l}"):
                        wait_x(both)

                ats_b, ats_c = ats_of(i - 1), ats_of(i - 2)
                update_c, old_c = upd[0:inner_rows, :], take(lat, ats_c)
                old_b, hidden_b, walls_c = take(lat, ats_b), take(hs, ats_b), walls_of(l, ats_c)
                new_c = latent_of(l, old_c, update_c)
                into = ats_c if l == 0 else ats_of(jnp.where(i < 2, face, i - 2))
                finish(l, into, inner_shape, new_c, walls_c)
                update_b = update_of(l, old_b, hidden_b)
                upd[0:inner_rows, :] = update_b
                for x in pair(i):
                    for y in range(1, ny - 1):
                        hs[x, y] = edges(l, x, y, range(6), None)

        with jax.named_scope(f"waity{l}"):
            wait_y(both)
        with jax.named_scope(f"by{l}"):
            ats_b, ats_c = ats_of(face), ats_of(face - 1)
            update_c, old_c = upd[0:inner_rows, :], take(lat, ats_c)
            old_b, hidden_b = take(lat, ats_b), take(hs, ats_b)
            update_b = update_of(l, old_b, hidden_b)
            new_c = latent_of(l, old_c, update_c)
            walls_c, walls_b = walls_of(l, ats_c), walls_of(l, ats_b)
            old_y, walls_y = take(lat, y_ats), walls_of(l, y_ats)
            for y in (0, ny - 1):
                for x in range(nx):
                    hs[x, y] = edges(l, x, y, range(6), None)
            finish(l, ats_c, inner_shape, new_c, walls_c)
            update_y = update_of(l, old_y, take(hs, y_ats))
            finish(l, ats_b, inner_shape, latent_of(l, old_b, update_b), walls_b)
            finish(l, y_ats, (nx, nz, h), latent_of(l, old_y, update_y), walls_y)
        with jax.named_scope(f"waits{l}"):
            wait_sent(both)

    with jax.named_scope("allred"):
        line[pl.ds(here["gz"], 1), 0:1, :] = jnp.sum(wall[...], axis=0, keepdims=True)[None]
        total = exchange(line, here["gz"], sizes["gz"], lambda j: {"gz": j}, 0)
        spot = here["gx"] * sizes["gy"] + here["gy"]
        plane[pl.ds(spot, 1)] = total[None]
        place = lambda j: {"gx": lax.div(j, sizes["gy"]), "gy": lax.rem(j, sizes["gy"])}
        total = exchange(plane, spot, sizes["gx"] * sizes["gy"], place, 1)
        out_wall[...] = total[0:1, :] / total[1:2, :]


def hand_over(latent, mean, out_latent, out_mean, sem):
    step = latent.shape[0] // PARTS
    parts = [pl.ds(k * step, step) for k in range(PARTS)]
    ways = [(mean, out_mean)] + [(latent.at[p], out_latent.at[p]) for p in parts]
    goes = [pltpu.make_async_copy(a, b, sem.at[k]) for k, (a, b) in enumerate(ways)]
    for g in goes:
        g.start()
    for g in goes:
        g.wait()


def solution(mesh):
    sizes = {a: mesh.shape[a] for a in AXES}

    def per_device(*args):
        args = list(args)
        args[8] = jnp.transpose(args[8], (1, 0, 2))
        args = [pltpu.with_memory_space_constraint(a, pltpu.HBM) for a in args]
        nx, ny, nz, h = dims = args[0].shape
        hbm = pl.BlockSpec(memory_space=pltpu.HBM)
        vmem = pl.BlockSpec(memory_space=pltpu.VMEM)
        latent, mean = pl.pallas_call(
            functools.partial(kernel, sizes, dims),
            out_shape=(
                jax.ShapeDtypeStruct(dims, BF),
                jax.ShapeDtypeStruct((1, h), F32),
            ),
            in_specs=[hbm] * 14,
            out_specs=(vmem, vmem),
            scratch_shapes=[pltpu.VMEM(a.shape, a.dtype) for a in args[1:]]
            + [
                pltpu.VMEM((nx + SPARE, ny, PITCH, h), F32),
                pltpu.VMEM((nx + SPARE, ny, PITCH, h), F32),
                pltpu.VMEM((nx * ny * nz // h, h), F32),
                pltpu.VMEM((2 * nx * nz, h), F32),
                pltpu.VMEM((8, h), F32),
                pltpu.VMEM((sizes["gz"], 2, h), F32),
                pltpu.VMEM((sizes["gx"] * sizes["gy"], 2, h), F32),
                pltpu.SemaphoreType.DMA((14,)),
                pltpu.SemaphoreType.DMA((2, 6)),
                pltpu.SemaphoreType.DMA((2, 6)),
                pltpu.SemaphoreType.DMA((2,)),
                pltpu.SemaphoreType.DMA((2,)),
            ],
            compiler_params=pltpu.CompilerParams(
                collective_id=0, has_side_effects=True, vmem_limit_bytes=48 * 1024 * 1024
            ),
            name="mesh_step",
        )(*args)
        latent, mean = pl.pallas_call(
            hand_over,
            out_shape=(
                jax.ShapeDtypeStruct(dims, BF),
                jax.ShapeDtypeStruct((1, h), F32),
            ),
            in_specs=[vmem, vmem],
            out_specs=(hbm, hbm),
            scratch_shapes=[
                pltpu.SemaphoreType.DMA((PARTS + 1,)),
            ],
            compiler_params=pltpu.CompilerParams(vmem_limit_bytes=16 * 1024 * 1024),
            name="hand_over",
        )(latent, mean)
        return latent, mean[0]

    block4 = P(*AXES, None)
    block3 = P(*AXES)
    return jax.shard_map(
        per_device,
        mesh=mesh,
        in_specs=(block4, block3, block3, block3) + (P(),) * 10,
        out_specs=(block4, P()),
        check_vma=False,
    )
```

time: 53.5 us -> 49.5 us (0.925)
  Pallas kernels: 52.7 us -> 48.7 us
    pallas_call x1, Pallas kernels: 50.3 us -> 47.3 us  [per_device(): pl.pallas_call(functools.partial(kernel, sizes, dims), out_shape=(jax.Sha...]
    pallas_call x1, Pallas kernels: 2.44 us -> 1.36 us  [per_device(): pl.pallas_call(hand_over, out_shape=(jax.ShapeDtypeStruct(dims, BF), jax....]
where the time goes in v2:
time: 49.5 us; the launch traced here: 49.3 us
  Pallas kernels  48.7 us (98%)
  between operations  0.64 us (1%)
    pallas_call x1, Pallas kernels, per_device(): pl.pallas_call(functools.partial(kernel, sizes, dims), out_shape=(jax.Sha...  47.3 us
    pallas_call x1, Pallas kernels, per_device(): pl.pallas_call(hand_over, out_shape=(jax.ShapeDtypeStruct(dims, BF), jax....  1.36 us

profile of v2, /device:TPU:1, one launch (start us, length us, event | category | flops | bytes accessed | tf_op | source)
XLA Modules:
  0.0 49.3 jit_solution(4821078714919006243)
XLA Ops:
  0.6 47.3 %mesh_step.1 = (bf16[16,16,32,128]{3,2,1,0:T(8,128)(2,1)S(1)}, f32[1,128]{1,0:T(1,128)S(1)}) custom-call(bf16[16,16,32,128]{3,2,1,0:T(8,128)(2,1)} %refs_0_.1, s32[16,16,32]{2,1,0:T(8,128)} %refs_1_.1, s32[16,16,32]{2,1,0:T(8,128)} %refs_2_.1, s32[16,16,32]{2,1,0:T(8,128)} %refs_3_.1, f32[4,128]{1,0:T(4,128)} %refs_4_.1, f32[3,128]{1,0:T(4,128)} %refs_5_.1, ...), custom_call_target="tpu_custom_call" | custom-call | tf_op jit(solution)/shard_map/mesh_step/pallas_call | solution.py:472
  48.0 1.4 %hand_over.1 = (bf16[16,16,32,128]{3,2,1,0:T(8,128)(2,1)}, f32[1,128]{1,0:T(1,128)}) custom-call(bf16[16,16,32,128]{3,2,1,0:T(8,128)(2,1)S(1)} %get-tuple-element.6.latent, f32[1,128]{1,0:T(1,128)S(1)} %get-tuple-element.7.mean), custom_call_target="tpu_custom_call" | custom-call | tf_op jit(solution)/shard_map/hand_over/pallas_call | solution.py:500

commit v3 on v2

--- a/solution.py
+++ b/solution.py
@@ -184,7 +184,10 @@
         new = (face + found).astype(BF)
         zsend[0, k] = matmul(new, w_sn[0, :, h:]).astype(BF).reshape(nx, ny, h)
 
-    def begin(rows, ats, shapes):
+    def take(ref, ats):
+        return jnp.concatenate([ref[at].reshape(-1, h) for at in ats], axis=0)
+
+    def look_up(rows, old):
         nodes = len(rows) * h
         nodes_code = jnp.concatenate([flat[pl.ds(r, 1), :] for r in rows], axis=1)
         nodes_code = jnp.broadcast_to(nodes_code, (2 * CODES, nodes))
@@ -196,16 +199,21 @@
         found = lax.dot_general(
             hot, tables[...], (((0,), (0,)), ((), ())), preferred_element_type=F32
         )
-        old = jnp.concatenate([lat[at].reshape(-1, h) for at in ats], axis=0)
-        new = (old.astype(F32) + found[:, :h]).astype(BF)
-        walls = found[:, h:].astype(BF)
-        both = matmul(new, w_sn[0])
+        return (old.astype(F32) + found[:, :h]).astype(BF), found[:, h:].astype(BF)
+
+    def pieces(ats, shapes):
         first = 0
         for at, shape in zip(ats, shapes, strict=True):
-            part = slice(first, first + shape[0] * nz)
+            yield at, shape, slice(first, first + shape[0] * nz)
             first += shape[0] * nz
+
+    def store_nodes(ats, shapes, new, walls):
+        for at, shape, part in pieces(ats, shapes):
             lat[at] = new[part].reshape(shape)
             mask[at] = walls[part].reshape(shape)
+
+    def store_projected(ats, shapes, both):
+        for at, shape, part in pieces(ats, shapes):
             store_parts(0, at, shape, both[part])
 
     def store_parts(r, at, shape, both):
@@ -307,11 +315,12 @@
             total = term if total is None else total + term
         return total
 
+    def edges_xy(l, x):
+        for y in range(1, ny - 1):
+            hs[x, y] = edges(l, x, y, (0, 1, 2, 3), None)
+
     def keep(cond):
         return jnp.full((nz, h), cond.astype(F32)).astype(BF)
-
-    def take(ref, ats):
-        return jnp.concatenate([ref[at].reshape(-1, h) for at in ats], axis=0)
 
     def update_of(l, old, hidden):
         p = matmul(jnp.concatenate([old, hidden], axis=1), w_pre[l]).astype(BF)
@@ -354,40 +363,56 @@
     travel = [copies(0), copies(1)]
     with jax.named_scope("prologue"):
 
-        @pl.loop(0, 2)
-        def _(c):
+        for c in range(2):
             half = nx // 2
-            xs = [half * c + k for k in range(half)]
+            xs = range(half * c, half * c + half)
             ats, shapes = [], []
             for x in xs:
                 ats += [(x, pl.ds(ny - 1, 1)), (x, pl.ds(0, per_row - 1))]
                 shapes += [(1, nz, h), (per_row - 1, nz, h)]
-            begin(xs, ats, shapes)
+            new, walls = look_up(xs, take(lat, ats))
+            store_nodes(ats, shapes, new, walls)
+            store_projected(ats, shapes, matmul(new, w_sn[0]))
 
         with jax.named_scope("bar"):
             pl.semaphore_wait(barrier, len(peers))
         start_z(travel[0])
         start_y(travel[0])
 
+        def two(i):
+            if isinstance(i, int):
+                return (2 * i - 1, 2 * i) if i > 0 else (0, nx - 1)
+            first = jnp.where(i == 0, 0, 2 * i - 1)
+            second = jnp.where(i == 0, nx - 1, 2 * i)
+            return jnp.where(i < 0, spare[0], first), jnp.where(i < 0, spare[1], second)
+
+        rest = (ny - per_row, nz, h)
+        rest_of = lambda xs: [(x, pl.ds(per_row - 1, ny - per_row)) for x in xs]
+
         @pl.loop(0, nx // 2)
         def _(i):
-            xs = (jnp.where(i == 0, 0, 2 * i - 1), jnp.where(i == 0, nx - 1, 2 * i))
-            rest = ny - per_row
+            xs = two(i)
+            ats, before = rest_of(xs), rest_of(two(i - 1))
+            done = take(lat, before)
             rows = [g * nx + x for x in xs for g in range(1, per_x)]
-            begin(rows, [(x, pl.ds(per_row - 1, rest)) for x in xs], [(rest, nz, h)] * 2)
-
-            @pl.when(i == 0)
+            new, walls = look_up(rows, take(lat, ats))
+            store_projected(before, [rest] * 2, matmul(done, w_sn[0]))
+            store_nodes(ats, [rest] * 2, new, walls)
+
+            @pl.when(i == 1)
             def _():
                 start_x(travel[0])
 
+        before = rest_of(two(nx // 2 - 1))
+        store_projected(before, [rest] * 2, matmul(take(lat, before), w_sn[0]))
         prepare(0)
 
     for l in range(2):
         both = travel[l]
         if l == 1:
             with jax.named_scope("start1"):
+                start_x(both)
                 start_y(both)
-                start_x(both)
                 zsend[1, 0] = sz1[0:nx, :, FIRST, :].astype(BF)
                 zsend[1, 1] = sz1[0:nx, :, FIRST + nz - 1, :].astype(BF)
                 start_z(both)
@@ -395,6 +420,13 @@
                 flags = ones_where(flat[...] >= CODES)
                 count = jnp.sum(jnp.sum(flags, axis=0, keepdims=True), axis=1, keepdims=True)
                 line[pl.ds(here["gz"], 1), 1:2, :] = jnp.broadcast_to(count, (1, h))[None]
+        if l == 1:
+            with jax.named_scope("pre1"):
+
+                @pl.loop(1, nx - 1)
+                def _(x):
+                    edges_xy(l, x)
+
         with jax.named_scope(f"waitz{l}"):
             wait_z(l, both)
         with jax.named_scope(f"main{l}"):
@@ -405,6 +437,12 @@
                 def _():
                     with jax.named_scope(f"waitx{l}"):
                         wait_x(both)
+
+                    if l == 1:
+
+                        @pl.loop(0, 2)
+                        def _(k):
+                            edges_xy(l, k * (nx - 1))
 
                 ats_b, ats_c = ats_of(i - 1), ats_of(i - 2)
                 update_c, old_c = upd[0:inner_rows, :], take(lat, ats_c)
@@ -416,7 +454,8 @@
                 upd[0:inner_rows, :] = update_b
                 for x in pair(i):
                     for y in range(1, ny - 1):
-                        hs[x, y] = edges(l, x, y, range(6), None)
+                        begun = hs[x, y] if l == 1 else None
+                        hs[x, y] = edges(l, x, y, (4, 5) if l == 1 else range(6), begun)
 
         with jax.named_scope(f"waity{l}"):
             wait_y(both)

time: 49.5 us -> 48 us (0.970)
  Pallas kernels: 48.7 us -> 47.3 us
    pallas_call x1, Pallas kernels: 47.3 us -> 45.9 us  [per_device(): pl.pallas_call(functools.partial(kernel, sizes, dims), out_shape=(jax.Sha...]
where the time goes in v3:
time: 48 us; the launch traced here: 47.9 us
  Pallas kernels  47.3 us (99%)
  between operations  0.64 us (1%)
    pallas_call x1, Pallas kernels, per_device(): pl.pallas_call(functools.partial(kernel, sizes, dims), out_shape=(jax.Sha...  45.9 us
    pallas_call x1, Pallas kernels, per_device(): pl.pallas_call(hand_over, out_shape=(jax.ShapeDtypeStruct(dims, BF), jax....  1.36 us

profile of v3, /device:TPU:1, one launch (start us, length us, event | category | flops | bytes accessed | tf_op | source)
XLA Modules:
  0.0 47.9 jit_solution(3126285943652089685)
XLA Ops:
  0.6 45.9 %mesh_step.1 = (bf16[16,16,32,128]{3,2,1,0:T(8,128)(2,1)S(1)}, f32[1,128]{1,0:T(1,128)S(1)}) custom-call(bf16[16,16,32,128]{3,2,1,0:T(8,128)(2,1)} %refs_0_.1, s32[16,16,32]{2,1,0:T(8,128)} %refs_1_.1, s32[16,16,32]{2,1,0:T(8,128)} %refs_2_.1, s32[16,16,32]{2,1,0:T(8,128)} %refs_3_.1, f32[4,128]{1,0:T(4,128)} %refs_4_.1, f32[3,128]{1,0:T(4,128)} %refs_5_.1, ...), custom_call_target="tpu_custom_call" | custom-call | tf_op jit(solution)/shard_map/mesh_step/pallas_call | solution.py:511
  46.6 1.4 %hand_over.1 = (bf16[16,16,32,128]{3,2,1,0:T(8,128)(2,1)}, f32[1,128]{1,0:T(1,128)}) custom-call(bf16[16,16,32,128]{3,2,1,0:T(8,128)(2,1)S(1)} %get-tuple-element.6.latent, f32[1,128]{1,0:T(1,128)S(1)} %get-tuple-element.7.mean), custom_call_target="tpu_custom_call" | custom-call | tf_op jit(solution)/shard_map/hand_over/pallas_call | solution.py:539

commit v4 on v3

--- a/solution.py
+++ b/solution.py
@@ -15,7 +15,7 @@
 PITCH = 48
 FIRST = 8
 PARTS = 4
-SPARE = 3
+SPARE = 5
 CODES = 16
 
 
@@ -108,7 +108,7 @@
         return total
 
     upd[...] = jnp.zeros_like(upd)
-    spare = (nx + 1, nx + 2)
+    spare = (nx + 1, nx + 2, nx + 3, nx + 4)
     for x in spare:
         for ref in (lat, hs, mask):
             ref[x] = jnp.zeros((ny, nz, h), BF)
@@ -379,40 +379,38 @@
         start_z(travel[0])
         start_y(travel[0])
 
-        def two(i):
+        def four(i):
+            first = (0, nx - 1, 1, 2)
             if isinstance(i, int):
-                return (2 * i - 1, 2 * i) if i > 0 else (0, nx - 1)
-            first = jnp.where(i == 0, 0, 2 * i - 1)
-            second = jnp.where(i == 0, nx - 1, 2 * i)
-            return jnp.where(i < 0, spare[0], first), jnp.where(i < 0, spare[1], second)
+                return first if i == 0 else tuple(4 * i - 1 + k for k in range(4))
+            later = [jnp.where(i == 0, first[k], 4 * i - 1 + k) for k in range(4)]
+            return tuple(jnp.where(i < 0, spare[k], x) for k, x in enumerate(later))
 
         rest = (ny - per_row, nz, h)
         rest_of = lambda xs: [(x, pl.ds(per_row - 1, ny - per_row)) for x in xs]
 
-        @pl.loop(0, nx // 2)
+        @pl.loop(0, nx // 4)
         def _(i):
-            xs = two(i)
-            ats, before = rest_of(xs), rest_of(two(i - 1))
+            xs = four(i)
+            ats, before = rest_of(xs), rest_of(four(i - 1))
             done = take(lat, before)
             rows = [g * nx + x for x in xs for g in range(1, per_x)]
             new, walls = look_up(rows, take(lat, ats))
-            store_projected(before, [rest] * 2, matmul(done, w_sn[0]))
-            store_nodes(ats, [rest] * 2, new, walls)
+            store_projected(before, [rest] * 4, matmul(done, w_sn[0]))
+            store_nodes(ats, [rest] * 4, new, walls)
 
             @pl.when(i == 1)
             def _():
                 start_x(travel[0])
 
-        before = rest_of(two(nx // 2 - 1))
-        store_projected(before, [rest] * 2, matmul(take(lat, before), w_sn[0]))
+        before = rest_of(four(nx // 4 - 1))
+        store_projected(before, [rest] * 4, matmul(take(lat, before), w_sn[0]))
         prepare(0)
 
     for l in range(2):
         both = travel[l]
         if l == 1:
             with jax.named_scope("start1"):
-                start_x(both)
-                start_y(both)
                 zsend[1, 0] = sz1[0:nx, :, FIRST, :].astype(BF)
                 zsend[1, 1] = sz1[0:nx, :, FIRST + nz - 1, :].astype(BF)
                 start_z(both)
@@ -470,10 +468,13 @@
             for y in (0, ny - 1):
                 for x in range(nx):
                     hs[x, y] = edges(l, x, y, range(6), None)
-            finish(l, ats_c, inner_shape, new_c, walls_c)
             update_y = update_of(l, old_y, take(hs, y_ats))
             finish(l, ats_b, inner_shape, latent_of(l, old_b, update_b), walls_b)
             finish(l, y_ats, (nx, nz, h), latent_of(l, old_y, update_y), walls_y)
+            if l == 0:
+                start_x(travel[1])
+                start_y(travel[1])
+            finish(l, ats_c, inner_shape, new_c, walls_c)
         with jax.named_scope(f"waits{l}"):
             wait_sent(both)
 

time: 48 us -> 47.8 us (level)
  no operation moved by 1% of the time
where the time goes in v4:
time: 47.8 us; the launch traced here: 47.7 us
  Pallas kernels  47.1 us (99%)
  between operations  0.64 us (1%)
    pallas_call x1, Pallas kernels, per_device(): pl.pallas_call(functools.partial(kernel, sizes, dims), out_shape=(jax.Sha...  45.7 us
    pallas_call x1, Pallas kernels, per_device(): pl.pallas_call(hand_over, out_shape=(jax.ShapeDtypeStruct(dims, BF), jax....  1.36 us

profile of v4, /device:TPU:1, one launch (start us, length us, event | category | flops | bytes accessed | tf_op | source)
XLA Modules:
  0.0 47.7 jit_solution(16516974471586164274)
XLA Ops:
  0.6 45.7 %mesh_step.1 = (bf16[16,16,32,128]{3,2,1,0:T(8,128)(2,1)S(1)}, f32[1,128]{1,0:T(1,128)S(1)}) custom-call(bf16[16,16,32,128]{3,2,1,0:T(8,128)(2,1)} %refs_0_.1, s32[16,16,32]{2,1,0:T(8,128)} %refs_1_.1, s32[16,16,32]{2,1,0:T(8,128)} %refs_2_.1, s32[16,16,32]{2,1,0:T(8,128)} %refs_3_.1, f32[4,128]{1,0:T(4,128)} %refs_4_.1, f32[3,128]{1,0:T(4,128)} %refs_5_.1, ...), custom_call_target="tpu_custom_call" | custom-call | tf_op jit(solution)/shard_map/mesh_step/pallas_call | solution.py:512
  46.4 1.4 %hand_over.1 = (bf16[16,16,32,128]{3,2,1,0:T(8,128)(2,1)}, f32[1,128]{1,0:T(1,128)}) custom-call(bf16[16,16,32,128]{3,2,1,0:T(8,128)(2,1)S(1)} %get-tuple-element.6.latent, f32[1,128]{1,0:T(1,128)S(1)} %get-tuple-element.7.mean), custom_call_target="tpu_custom_call" | custom-call | tf_op jit(solution)/shard_map/hand_over/pallas_call | solution.py:540
